TPU v7x, 32 devices: a whole 2x2x4 slice. The times are simulated.
32 devices in a mesh: row: 4 (over y, x), col: 8 (over z, core).
Axes of the slice: x: 2, y: 2, z: 4, core: 2. Of those that a mesh axis runs over, the one named last changes fastest.
Arguments:
- points: bfloat16 [10240, 64], P(('row', 'col')), may hold values from -5 to 5
- start_vectors: bfloat16 [10240, 32], P(('row', 'col')), may hold values from -12 to 12
Outputs:
- basis: float32 [10240, 32], P(('row', 'col'))
All inputs are finite; a program needn't handle non-finite values.
Results may differ from a plain program's by a relative error of at most 0.007.
Values may be sent and summed in bfloat16 or wider, within the bound.
A program may use at most 64 MiB of HBM per device.

v0:
```python
import jax
import jax.numpy as jnp
from jax import lax
from jax.sharding import PartitionSpec as P

ITERS = 2


KERNEL_SCALE = 5.12


def squared_norms(values):
    return jnp.sum(jnp.square(values.astype(jnp.float32)), axis=1)


def affinity(block_pts, block_sq, col_pts, col_sq):
    features = block_pts.shape[1]
    cross = lax.dot_general(
        block_pts, col_pts, (((1,), (1,)), ((), ())), preferred_element_type=jnp.float32
    )
    dist = block_sq[:, None] + col_sq[None, :] - 2.0 * cross
    return jnp.exp(dist * (-KERNEL_SCALE / features)).astype(jnp.bfloat16)


def sweep(row_pts, row_sq, col_pts, col_sq, panel, with_degree):
    rows, features = row_pts.shape
    height = min(512, rows)
    count = rows // height
    stacked = (row_pts.reshape(count, height, features), row_sq.reshape(count, height))

    def one_block(item):
        weights = affinity(item[0], item[1], col_pts, col_sq)
        results = ()
        if panel is not None:
            results = results + (jnp.dot(weights, panel, preferred_element_type=jnp.float32),)
        if with_degree:
            results = results + (jnp.sum(weights, axis=1, dtype=jnp.float32),)
        return results

    mapped = lax.map(one_block, stacked)
    return [piece.reshape((rows,) + piece.shape[2:]) for piece in mapped]


def orthonormal(product, degree, total):
    scaled = product / degree[:, None]
    gram_part = jnp.dot(
        scaled.T, scaled, precision=lax.Precision.HIGHEST, preferred_element_type=jnp.float32
    )
    gram = lax.psum(gram_part, ("row", "col"))
    lower = jnp.linalg.cholesky(gram / total)
    return lax.linalg.triangular_solve(lower, scaled, left_side=False, lower=True, transpose_a=True)


def shards(points, start_vectors):
    group = points.shape[0]
    total = group * lax.axis_size("row") * lax.axis_size("col")
    row_pts = lax.all_gather(points, "col", axis=0, tiled=True)
    col_pts = lax.all_gather(points, "row", axis=0, tiled=True)
    row_sq = squared_norms(row_pts)
    col_sq = squared_norms(col_pts)
    degree_part = sweep(row_pts, row_sq, col_pts, col_sq, None, True)[0]
    vectors = start_vectors
    ortho = jnp.zeros(start_vectors.shape, jnp.float32)
    degree = None
    for step in range(ITERS):
        panel = lax.all_gather(vectors, "row", axis=0, tiled=True)
        if step == 0:
            product_part = sweep(row_pts, row_sq, col_pts, col_sq, panel, False)[0]
            product, degree = (
                lax.psum_scatter(product_part, "col", scatter_dimension=0, tiled=True),
                lax.psum_scatter(degree_part, "col", scatter_dimension=0, tiled=True),
            )
        else:
            product_part = sweep(row_pts, row_sq, col_pts, col_sq, panel, False)[0]
            product = lax.psum_scatter(product_part, "col", scatter_dimension=0, tiled=True)
        ortho = orthonormal(product, degree, total)
        vectors = ortho.astype(jnp.bfloat16)
    return ortho


def solution(mesh):
    return jax.shard_map(
        shards,
        mesh=mesh,
        in_specs=(P(("row", "col"), None), P(("row", "col"), None)),
        out_specs=P(("row", "col"), None),
        check_vma=False,
    )
```

profile of v0, /device:TPU:0, one launch (start us, length us, event | category | flops | bytes accessed | tf_op | source)
XLA Modules:
  0.0 230.3 jit_solution(14613255640322226920)
XLA Ops:
  6.5 16.4 %all-gather = bf16[8,320,64]{1,2,0:T(8,128)(2,1)S(1)} all-gather(bf16[1,320,64]{1,2,0:T(8,128)(2,1)} %bitcast.101), channel_id=1, replica_groups=mesh['row'=4,'col'=8] {'col'}, dimensions={0}, use_global_device_ids=true | all-gather | bytes 368640 | tf_op jit(solution)/shard_map/all_gather | solution.py:57
  23.0 9.0 %all-gather.1 = bf16[4,320,64]{1,2,0:T(8,128)(2,1)S(1)} all-gather(bf16[1,320,64]{1,2,0:T(8,128)(2,1)} %bitcast.102), channel_id=1, replica_groups=mesh['row'=4,'col'=8] {'row'}, dimensions={0}, use_global_device_ids=true | all-gather | bytes 204800 | tf_op jit(solution)/shard_map/all_gather | solution.py:58
  32.3 0.2 copy.42
  32.5 0.3 copy.55
  33.1 8.1 %all-gather.2 = bf16[4,320,32]{1,2,0:T(8,128)(2,1)S(1)} all-gather(bf16[1,320,32]{1,2,0:T(8,128)(2,1)S(1)} %bitcast.107), channel_id=1, replica_groups=mesh['row'=4,'col'=8] {'row'}, dimensions={0}, use_global_device_ids=true | all-gather | bytes 102400 | tf_op jit(solution)/shard_map/all_gather | solution.py:66
  41.1 0.2 copy.49
  41.4 4.9 %while.30 = (s32[]{:T(128)}, f32[5,512,32]{1,2,0:T(8,128)S(1)}, f32[5,512]{1,0:T(8,128)S(1)}, f32[1280]{0:T(1024)S(1)}, bf16[5,512,64]{2,1,0:T(8,128)(2,1)S(1)},...) while((s32[]{:T(128)}, f32[5,512,32]{1,2,0:T(8,128)S(1)}, ...), condition=%wide.region_3.4_spmd, body=%wide.region_2.3_spmd.sunk | while | flops 129105920 | bytes 867417 | solution.py:40
  41.4 1.0 fusion.78
  42.4 1.0 fusion.78
  43.4 1.0 fusion.78
  44.4 1.0 fusion.78
  45.4 1.0 fusion.78
  46.3 1.5 copy.58
  47.9 4.8 %while.31 = (s32[]{:T(128)}, f32[5,512]{1,0:T(8,128)S(1)}, f32[5,512]{1,0:T(8,128)S(1)}, f32[1280]{0:T(1024)S(1)}, bf16[5,512,64]{2,1,0:T(8,128)(2,1)S(1)}, /*in...) while((s32[]{:T(128)}, f32[5,512]{1,0:T(8,128)S(1)}, f32[5,512]{1,0:T(8,128)S(1)}, f32[1280]{0:T(1024)S(1)}, ...), condition=%wide.region_7.8_spmd, body=%wide.region_5.7_spmd.sunk | while | flops 88473088 | bytes 479329 | solution.py:40
  47.9 0.9 fusion.81
  48.9 0.9 fusion.81
  49.8 0.9 fusion.81
  50.8 0.9 fusion.81
  51.7 0.9 fusion.81
  52.7 0.6 dynamic-slice
  53.9 25.9 %all-reduce = f32[2560]{0:T(1024)S(1)} all-reduce(f32[2560]{0:T(1024)S(1)} %reshape.43), channel_id=3, replica_groups=mesh['row'=4,'col'=8] {'col'}, use_global_device_ids=true, to_apply=%region_8.9.clone | all-reduce | flops 2560 | bytes 20480
  79.9 1.5 reduce-scatter.7.cloned.1.call-done
  81.5 1.0 copy.52
  82.5 0.2 fusion.49
  82.7 37.8 %psum.14 = f32[32,32]{0,1:T(8,128)S(1)} all-reduce(f32[32,32]{0,1:T(8,128)S(1)} %fusion.49), channel_id=1, replica_groups=mesh['row'=4,'col'=8] {'row','col'}, use_global_device_ids=true, to_apply=%region_9.10 | all-reduce | flops 1024 | bytes 8192 | tf_op jit(solution)/shard_map/psum | solution.py:49
  120.6 2.9 %cholesky.44 = f32[32,32]{1,0:T(8,128)S(1)} custom-call(f32[32,32]{1,0:T(8,128)S(1)} %fusion.56), custom_call_target="Cholesky" | custom-call | tf_op jit(solution)/shard_map/jit(cholesky)/cholesky | solution.py:50
  123.6 0.7 compare_reduce_fusion.1
  124.3 0.7 fusion.51
  125.0 2.4 %custom-call.6 = f32[1,32,32]{1,2,0:T(8,128)S(1)} custom-call(f32[1,32,32]{2,1,0:T(8,128)S(1)} %fusion.51), custom_call_target="InvertDiagBlocksLowerTriangular" | custom-call | tf_op jit(solution)/shard_map/triangular_solve/custom-call.0 | solution.py:51
  127.4 0.3 fusion.48
  127.7 9.1 %all-gather.3 = bf16[4,320,32]{1,2,0:T(8,128)(2,1)S(1)} all-gather(bf16[1,320,32]{1,2,0:T(8,128)(2,1)S(1)} %fusion.48), channel_id=1, replica_groups=mesh['row'=4,'col'=8] {'row'}, dimensions={0}, use_global_device_ids=true | all-gather | bytes 102400 | tf_op jit(solution)/shard_map/all_gather | solution.py:66
  136.9 0.2 copy.50
  137.1 4.9 %while.32 = (s32[]{:T(128)}, f32[5,512,32]{1,2,0:T(8,128)S(1)}, f32[5,512]{1,0:T(8,128)S(1)}, f32[1280]{0:T(1024)S(1)}, bf16[5,512,64]{2,1,0:T(8,128)(2,1)S(1)},...) while((s32[]{:T(128)}, f32[5,512,32]{1,2,0:T(8,128)S(1)}, ...), condition=%wide.region_13.16_spmd, body=%wide.region_12.15_spmd.sunk | while | flops 129105920 | bytes 867417 | solution.py:40
  137.2 1.0 fusion.85
  138.1 1.0 fusion.85
  139.1 1.0 fusion.85
  140.1 1.0 fusion.85
  141.1 1.0 fusion.85
  142.0 1.5 copy.60
  143.5 33.0 %reduce-scatter.9.cloned.1.call-done = f32[320,32]{1,0:T(8,128)} async-done(((f32[2560,32]{1,0:T(8,128)}), f32[320,32]{1,0:T(8,128)}) %reduce-scatter.9.cloned.1.call-update) | async-done | bytes 40976
  176.5 1.0 copy.54
  177.5 0.2 fusion.50
  177.7 38.0 %psum.15 = f32[32,32]{0,1:T(8,128)S(1)} all-reduce(f32[32,32]{0,1:T(8,128)S(1)} %fusion.50), channel_id=1, replica_groups=mesh['row'=4,'col'=8] {'row','col'}, use_global_device_ids=true, to_apply=%region_15.18 | all-reduce | flops 1024 | bytes 8192 | tf_op jit(solution)/shard_map/psum | solution.py:49
  215.9 2.9 %cholesky.55 = f32[32,32]{1,0:T(8,128)S(1)} custom-call(f32[32,32]{1,0:T(8,128)S(1)} %fusion.54), custom_call_target="Cholesky" | custom-call | tf_op jit(solution)/shard_map/jit(cholesky)/cholesky | solution.py:50
  218.8 0.6 compare_reduce_fusion
  219.5 0.7 fusion.52
  220.1 2.4 %custom-call.7 = f32[1,32,32]{1,2,0:T(8,128)S(1)} custom-call(f32[1,32,32]{2,1,0:T(8,128)S(1)} %fusion.52), custom_call_target="InvertDiagBlocksLowerTriangular" | custom-call | tf_op jit(solution)/shard_map/triangular_solve/custom-call.0 | solution.py:51
  222.6 0.9 convolution_bitcast_fusion
  (46 shorter events, 1.4 us)
Async XLA Ops:
  6.5 74.9 %reduce-scatter.7.cloned.1.call-start = ((), (), s32[]{:S(2)}) async-start(), calls=%async_computation.2 | async-start | bytes 1474560
  32.1 1.0 copy-start
  47.8 128.7 %reduce-scatter.9.cloned.1.call-start = ((), (), s32[]{:S(2)}) async-start(), calls=%async_computation.3 | async-start | bytes 1474560
  47.9 4.8 %copy-start.1 = (u32[32]{0:T(128)S(1)}, u32[32]{0:T(128)}, u32[]{:S(2)}) copy-start(u32[32]{0:T(128)} %constant.83) | copy-start | bytes 388
Sparse Core Ops, SparseCore 0:
  47.9 33.4 reduce-scatter.6
  143.7 32.8 reduce-scatter.8
where the time goes:
time: 231 us; the launch traced here: 230 us
  blocking collectives  144 us (62%)
  waiting for transfers between devices  34.5 us (15%)
  matrix products  15.5 us (7%)
  between operations  14.2 us (6%)
  other arithmetic  13.7 us (6%)
  local copies, waits for them, and re-layouts  7.68 us (3%)
    psum x2, blocking collectives, orthonormal(): gram = lax.psum(gram_part, ('row', 'col'))  75.9 us
    unnamed x4, waiting for transfers between devices  34.5 us
    unnamed x1, blocking collectives  25.9 us
    all_gather x2, blocking collectives, shards(): panel = lax.all_gather(vectors, 'row', axis=0, tiled=True)  17.2 us
    all_gather x1, blocking collectives, shards(): row_pts = lax.all_gather(points, 'col', axis=0, tiled=True)  16.4 us
    dot_general x10, matrix products, one_block(): jnp.dot(weights, panel, preferred_element_type=jnp.float32)  9.6 us
    all_gather x1, blocking collectives, shards(): col_pts = lax.all_gather(points, 'row', axis=0, tiled=True)  8.96 us
    another operation x6, other arithmetic, orthonormal(): lower = jnp.linalg.cholesky(gram / total)  7.27 us
  transfers between devices with their start and end apart: 2, of which 2 were waited for; matrix products, arithmetic and copies ran while one was open for 2% of the time, Pallas kernels for 0%

commit v1 on v0

v1 whole, which is shorter than its diff:
```python
import functools

import jax
import jax.numpy as jnp
from jax import lax
from jax.experimental import pallas as pl
from jax.experimental.pallas import tpu as pltpu
from jax.sharding import PartitionSpec as P

KERNEL_SCALE = 5.12
LOG2E = 1.4426950408889634
MESH = pl.DeviceIdType.MESH
HIGHEST = lax.Precision.HIGHEST
LANES = 128


def packing(rows):
    for stacks in (4, 2, 1):
        if rows % (16 * stacks) == 0:
            return stacks
    raise ValueError(rows)


def width(stacks, lanes):
    return -(-stacks * lanes // LANES) * LANES


def side_by_side(value, stacks):
    rows, lanes = value.shape
    high = rows // stacks
    pieces = [value[s * high : (s + 1) * high] for s in range(stacks)]
    spare = width(stacks, lanes) - stacks * lanes
    if spare:
        pieces.append(jnp.zeros((high, spare), value.dtype))
    return jnp.concatenate(pieces, axis=1)


def inverse_factor(gram):
    size = gram.shape[0]
    down = lax.broadcasted_iota(jnp.int32, (size, size), 0)
    across = lax.broadcasted_iota(jnp.int32, (size, size), 1)
    unit = (down == across).astype(jnp.float32)
    work = jnp.concatenate([gram, unit], axis=1)
    below = lax.broadcasted_iota(jnp.int32, (size, 1), 0)
    for k in range(size - 1):
        row = work[k : k + 1, :]
        factor = work[:, k : k + 1] * (1.0 / work[k : k + 1, k : k + 1])
        work = work - jnp.where(below > k, factor, 0.0) * row
    pivots = jnp.sum(work[:, :size] * unit, axis=1, keepdims=True)
    return work[:, size:] * lax.rsqrt(pivots)


def kernel(nrow, ncol, total, pts_ref, vec_ref, out_ref, gp, gv, gs, aff, acc,
           gram_col, gram_row, sems_p, sems_v, sems_s, sems_g):
    row, col = lax.axis_index("row"), lax.axis_index("col")
    nz = ncol // 2
    z, core = col // 2, col % 2
    sibling = z * 2 + (1 - core)
    rows, features = pts_ref.shape
    vectors = vec_ref.shape[1]
    stacks = packing(rows)
    high = rows // stacks
    per_tile = max(1, LANES // features)

    def row_at(j):
        return lax.rem(row + j, nrow)

    def col_at(k):
        return lax.rem(z + k, nz) * 2 + core

    def view(buf, r, c):
        return buf.at[r, pl.ds(pl.multiple_of(c * high, high), high)]

    def block(buf, r, c, send, recv, to_row, to_col):
        return pltpu.make_async_remote_copy(
            src_ref=view(buf, r, c), dst_ref=view(buf, r, c), send_sem=send, recv_sem=recv.at[r, c],
            device_id=(to_row, to_col), device_id_type=MESH,
        )

    def arrived(gather, r, c):
        buf, recv, along, spread, pair = gather
        block(buf, r, c, pair.at[0, 0], recv, row, sibling).wait_recv()

    def hand_over(gather, j, k):
        buf, recv, along, spread, pair = gather
        block(buf, row_at(j), col_at(k), pair.at[j, k], recv, row, sibling).start()

    def send_plane(gather, k):
        buf, recv, along, spread, pair = gather
        for j in range(1, nrow):
            block(buf, row, col_at(k), spread.at[k, j - 1], recv, row_at(j), col).start()
        hand_over(gather, 0, k)

    def send_own(gather):
        buf, recv, along, spread, pair = gather
        for k in range(1, nz):
            block(buf, row, col, along.at[k - 1], recv, row, col_at(k)).start()
        send_plane(gather, 0)

    def pass_on(gather):
        for k in range(1, nz):
            arrived(gather, row, col_at(k))
            send_plane(gather, k)

    def hand_over_row(gather, j):
        for k in range(nz):
            arrived(gather, row_at(j), col_at(k))
            hand_over(gather, j, k)

    def sibling_row(gather, j):
        for k in range(nz):
            arrived(gather, row_at(j), lax.rem(z + k, nz) * 2 + (1 - core))

    def drain(gather):
        buf, recv, along, spread, pair = gather
        for k in range(1, nz):
            block(buf, row, col, along.at[k - 1], recv, row, col_at(k)).wait_send()
        for k in range(nz):
            for j in range(1, nrow):
                block(buf, row, col_at(k), spread.at[k, j - 1], recv, row_at(j), col).wait_send()
            for j in range(nrow):
                block(buf, row_at(j), col_at(k), pair.at[j, k], recv, row, sibling).wait_send()

    points = (gp,) + tuple(sems_p)
    start = (gv,) + tuple(sems_v)
    middle = (gs,) + tuple(sems_s)

    barrier = pltpu.get_barrier_semaphore()
    for j in range(1, nrow):
        pl.semaphore_signal(barrier, inc=1, device_id=(row_at(j), col), device_id_type=MESH)
    for k in range(1, ncol):
        pl.semaphore_signal(barrier, inc=1, device_id=(row, lax.rem(col + k, ncol)), device_id_type=MESH)

    own = pl.ds(pl.multiple_of(col * high, high), high)
    x = pts_ref[...]
    gp[row, own, :] = side_by_side(x, stacks)
    gv[row, own, :] = side_by_side(vec_ref[...], stacks)
    pl.semaphore_wait(barrier, nrow + ncol - 2)

    send_own(points)
    send_own(start)

    rate = -KERNEL_SCALE / features * LOG2E
    xf = x.astype(jnp.float32)
    here = jnp.sum(xf * xf, axis=1, keepdims=True) * rate
    blank = jnp.zeros_like(x)
    left = []
    for s in range(per_tile):
        parts = [x if s == t else blank for t in range(per_tile)]
        left.append(jnp.concatenate(parts, axis=1))
    lane = lax.broadcasted_iota(jnp.int32, (8 * per_tile, LANES), 1)
    down = lax.broadcasted_iota(jnp.int32, (8 * per_tile, LANES), 0)
    picks = (lane // features == down // 8).astype(jnp.bfloat16)
    contract = (((1,), (1,)), ((), ()))

    def weights(r):
        for s in range(stacks):
            tile, part = s // per_tile, s % per_tile
            right = gp[r, :, tile * LANES : (tile + 1) * LANES]
            if part == 0:
                wide = right.astype(jnp.float32)
                square = wide * wide
                upper = square.astype(jnp.bfloat16)
                lower = (square - upper.astype(jnp.float32)).astype(jnp.bfloat16)
                there = (
                    lax.dot_general(picks, upper, contract, preferred_element_type=jnp.float32)
                    + lax.dot_general(picks, lower, contract, preferred_element_type=jnp.float32)
                ) * rate
            cross = lax.dot_general(left[part], right, contract, preferred_element_type=jnp.float32)
            power = (cross * (-2.0 * rate) + there[8 * part : 8 * part + 1]) + here
            aff[r, s] = jnp.exp2(power).astype(jnp.bfloat16)

    pass_on(points)
    pass_on(start)
    sibling_row(points, 0)
    weights(row)

    def next_row(j, carry):
        hand_over_row(points, j)
        sibling_row(points, j)
        weights(row_at(j))
        return carry

    lax.fori_loop(1, nrow, next_row, 0)

    span = gv.shape[2]
    ones = jnp.ones((ncol * high, LANES), jnp.bfloat16)
    acc[...] = jnp.zeros_like(acc)

    def first_row(j, carry):
        sibling_row(start, j)
        r = row_at(j)
        panel = jnp.concatenate([gv[r], ones], axis=1)
        for s in range(stacks):
            acc[s] += jnp.dot(aff[r, s], panel, preferred_element_type=jnp.float32)
        return carry

    def hand_over_start(j, carry):
        hand_over_row(start, j)
        return carry

    lax.fori_loop(1, nrow, hand_over_start, 0)
    lax.fori_loop(0, nrow, first_row, 0)

    product = sum(acc[s][:, s * vectors : (s + 1) * vectors] for s in range(stacks))
    degree = sum(acc[s][:, span : span + vectors] for s in range(stacks))
    scaled = product / degree
    gs[row, own, :] = side_by_side(scaled.astype(jnp.bfloat16), stacks)
    send_own(middle)

    folds = LANES // vectors
    tall = vectors // folds

    def gram_send(step, value):
        part = jnp.dot(value.T, value, precision=HIGHEST, preferred_element_type=jnp.float32) * (1.0 / total)
        gram_col[step, col] = jnp.concatenate([part[f * tall : (f + 1) * tall] for f in range(folds)], axis=1)
        for k in range(1, ncol):
            gram_copy(gram_col, step, col, k - 1, row, lax.rem(col + k, ncol), 0).start()

    def gram_copy(buf, step, slot, k, to_row, to_col, axis):
        return pltpu.make_async_remote_copy(
            src_ref=buf.at[step, slot], dst_ref=buf.at[step, slot],
            send_sem=sems_g[2 * axis].at[step, k], recv_sem=sems_g[2 * axis + 1].at[step, slot],
            device_id=(to_row, to_col), device_id_type=MESH,
        )

    def gram_across(step):
        for k in range(1, ncol):
            slot = lax.rem(col + k, ncol)
            gram_copy(gram_col, step, slot, k - 1, row, slot, 0).wait_recv()
        gram_row[step, row] = sum(gram_col[step, c] for c in range(ncol))
        for j in range(1, nrow):
            gram_copy(gram_row, step, row, j - 1, row_at(j), col, 1).start()

    def gram_whole(step):
        for j in range(1, nrow):
            gram_copy(gram_row, step, row_at(j), j - 1, row_at(j), col, 1).wait_recv()
        flat = sum(gram_row[step, r] for r in range(nrow))
        return jnp.concatenate([flat[:, f * vectors : (f + 1) * vectors] for f in range(folds)], axis=0)

    def gram_drain(step):
        for k in range(1, ncol):
            gram_copy(gram_col, step, col, k - 1, row, lax.rem(col + k, ncol), 0).wait_send()
        for j in range(1, nrow):
            gram_copy(gram_row, step, row, j - 1, row_at(j), col, 1).wait_send()

    gram_send(0, scaled)
    pass_on(middle)
    gram_across(0)
    first = inverse_factor(gram_whole(0))

    def hand_over_middle(j, carry):
        hand_over_row(middle, j)
        return carry

    def second_row(j, carry):
        sibling_row(middle, j)
        r = row_at(j)
        for s in range(stacks):
            acc[s, :, :span] += jnp.dot(aff[r, s], gs[r], preferred_element_type=jnp.float32)
        return carry

    acc[...] = jnp.zeros_like(acc)
    lax.fori_loop(1, nrow, hand_over_middle, 0)
    lax.fori_loop(0, nrow, second_row, 0)
    product = sum(acc[s][:, s * vectors : (s + 1) * vectors] for s in range(stacks))
    scaled = lax.dot_general(
        product / degree, first, contract, precision=HIGHEST, preferred_element_type=jnp.float32
    )
    gram_send(1, scaled)
    drain(points)
    drain(start)
    drain(middle)
    gram_drain(0)
    gram_across(1)
    second = inverse_factor(gram_whole(1))
    out_ref[...] = lax.dot_general(scaled, second, contract, precision=HIGHEST, preferred_element_type=jnp.float32)
    gram_drain(1)


def solution(mesh):
    nrow, ncol = mesh.shape["row"], mesh.shape["col"]
    nz = ncol // 2

    def step(points, start_vectors):
        rows, features = points.shape
        vectors = start_vectors.shape[1]
        stacks = packing(rows)
        high = rows // stacks
        wide, span = width(stacks, features), width(stacks, vectors)
        dma = pltpu.SemaphoreType.DMA
        gather = [dma((nrow, ncol)), dma((nz,)), dma((nz, nrow)), dma((nrow, nz))]
        tall = vectors * vectors // LANES
        return pl.pallas_call(
            functools.partial(kernel, nrow, ncol, rows * nrow * ncol),
            out_shape=jax.ShapeDtypeStruct((rows, vectors), jnp.float32),
            in_specs=[pl.BlockSpec(memory_space=pltpu.VMEM)] * 2,
            out_specs=pl.BlockSpec(memory_space=pltpu.VMEM),
            scratch_shapes=[
                pltpu.VMEM((nrow, ncol * high, wide), jnp.bfloat16),
                pltpu.VMEM((nrow, ncol * high, span), jnp.bfloat16),
                pltpu.VMEM((nrow, ncol * high, span), jnp.bfloat16),
                pltpu.VMEM((nrow, stacks, rows, ncol * high), jnp.bfloat16),
                pltpu.VMEM((stacks, rows, span + LANES), jnp.float32),
                pltpu.VMEM((2, ncol, tall, LANES), jnp.float32),
                pltpu.VMEM((2, nrow, tall, LANES), jnp.float32),
                gather, gather, gather,
                [dma((2, ncol)), dma((2, ncol)), dma((2, nrow)), dma((2, nrow))],
            ],
            compiler_params=pltpu.CompilerParams(
                collective_id=0, has_side_effects=True, vmem_limit_bytes=56 * 1024 * 1024
            ),
        )(points, start_vectors)

    return jax.shard_map(
        step,
        mesh=mesh,
        in_specs=(P(("row", "col"), None), P(("row", "col"), None)),
        out_specs=P(("row", "col"), None),
        check_vma=False,
    )
```

time: 231 us -> 60.5 us (0.26)
  blocking collectives: 144 us -> 0 us
  Pallas kernels: 0 us -> 56.3 us
  waiting for transfers between devices: 34.5 us -> 0 us
  matrix products: 15.5 us -> 0 us
  between operations: 14.2 us -> 0.01 us
  other arithmetic: 13.7 us -> 0 us
  local copies, waits for them, and re-layouts: 7.68 us -> 3.92 us
    psum x2 -> x0, blocking collectives: 75.9 us -> none  [orthonormal(): gram = lax.psum(gram_part, ('row', 'col'))]
    pallas_call x0 -> x1, Pallas kernels: none -> 56.3 us  [step(): pl.pallas_call(functools.partial(kernel, nrow, ncol, rows * nrow * ncol),...]
    all_gather x4 -> x0, blocking collectives: 42.6 us -> none  [the longest x2 17.2 us: shards(): panel = lax.all_gather(vectors, 'row', axis=0, tiled=True)]
    unnamed x4 -> x0, waiting for transfers between devices: 34.5 us -> none
    unnamed x1 -> x0, blocking collectives: 25.9 us -> none
    dot_general x17 -> x0, matrix products: 14.3 us -> none  [the longest x10 9.6 us: one_block(): jnp.dot(weights, panel, preferred_element_type=jnp.float32)]
    another operation x10 -> x0, other arithmetic: 13.5 us -> none  [the longest x6 7.27 us: orthonormal(): lower = jnp.linalg.cholesky(gram / total)]
    unnamed x10 -> x4, local copies, waits for them, and re-layouts: 5.66 us -> 2.28 us
  transfers between devices with their start and end apart: 2 -> 0, of which waited for: 2 -> 0; matrix products, arithmetic and copies ran while one was open for 2% -> 0% of each run, Pallas kernels for 0% -> 0%
where the time goes in v1:
time: 60.5 us; the launch traced here: 60.3 us
  Pallas kernels  56.3 us (93%)
  local copies, waits for them, and re-layouts  3.92 us (6%)
    pallas_call x1, Pallas kernels, step(): pl.pallas_call(functools.partial(kernel, nrow, ncol, rows * nrow * ncol),...  56.3 us
    unnamed x4, local copies, waits for them, and re-layouts  2.28 us
    pallas_call x1, local copies, waits for them, and re-layouts, step(): pl.pallas_call(functools.partial(kernel, nrow, ncol, rows * nrow * ncol),...  1.64 us

profile of v1, /device:TPU:0, one launch (start us, length us, event | category | flops | bytes accessed | tf_op | source)
XLA Modules:
  0.0 60.3 jit_solution(6778255904304827007)
XLA Ops:
  0.0 0.0 copy-start
  0.0 1.5 %copy.3.pts_ref = bf16[320,64]{1,0:T(8,128)(2,1)} copy(bf16[320,64]{0,1:T(8,128)(2,1)} %param.2) | data formatting | bytes 81920 | tf_op args[0]
  1.5 0.0 copy-done
  1.5 0.7 %copy.4.vec_ref = bf16[320,32]{1,0:T(8,128)(2,1)} copy(bf16[320,32]{0,1:T(8,128)(2,1)S(1)} %copy-done) | data formatting | bytes 40960 | tf_op args[1]
  2.3 56.3 %shard_map.28 = f32[320,32]{1,0:T(8,128)} custom-call(bf16[320,64]{1,0:T(8,128)(2,1)} %copy.3.pts_ref, bf16[320,32]{1,0:T(8,128)(2,1)} %copy.4.vec_ref), custom_call_target="tpu_custom_call" | custom-call | tf_op jit(solution)/shard_map/pallas_call | solution.py:294
  58.6 1.6 %copy.5 = f32[320,32]{0,1:T(8,128)} copy(f32[320,32]{1,0:T(8,128)} %shard_map.28) | data formatting | bytes 81920 | tf_op jit(solution)/shard_map/pallas_call | solution.py:294
Async XLA Ops:
  0.0 1.5 %copy-start = (bf16[320,32]{0,1:T(8,128)(2,1)S(1)}, bf16[320,32]{0,1:T(8,128)(2,1)}, u32[]{:S(2)}) copy-start(bf16[320,32]{0,1:T(8,128)(2,1)} %param.3) | copy-start | bytes 61444

commit v2 on v1

--- a/solution.py
+++ b/solution.py
@@ -19,6 +19,17 @@
         if rows % (16 * stacks) == 0:
             return stacks
     raise ValueError(rows)
+
+
+def square_side(count):
+    side = 1
+    while side * side < count:
+        side += 1
+    return side if side * side == count else count
+
+
+def upright(value):
+    return value.astype(jnp.float32).T.astype(value.dtype)
 
 
 def width(stacks, lanes):
@@ -41,11 +52,16 @@
     across = lax.broadcasted_iota(jnp.int32, (size, size), 1)
     unit = (down == across).astype(jnp.float32)
     work = jnp.concatenate([gram, unit], axis=1)
-    below = lax.broadcasted_iota(jnp.int32, (size, 1), 0)
-    for k in range(size - 1):
-        row = work[k : k + 1, :]
-        factor = work[:, k : k + 1] * (1.0 / work[k : k + 1, k : k + 1])
-        work = work - jnp.where(below > k, factor, 0.0) * row
+    below = lax.broadcasted_iota(jnp.int32, work.shape, 0)
+    panel = 8
+    for first in range(0, size, panel):
+        columns = [jnp.broadcast_to(work[:, k : k + 1], work.shape) for k in range(first, first + panel)]
+        for m in range(panel):
+            k = first + m
+            factor = jnp.where(below > k, columns[m] * (1.0 / columns[m][k : k + 1]), 0.0)
+            work = work - factor * work[k : k + 1]
+            for later in range(m + 1, panel):
+                columns[later] = columns[later] - factor * columns[later][k : k + 1]
     pivots = jnp.sum(work[:, :size] * unit, axis=1, keepdims=True)
     return work[:, size:] * lax.rsqrt(pivots)
 
@@ -56,14 +72,19 @@
     nz = ncol // 2
     z, core = col // 2, col % 2
     sibling = z * 2 + (1 - core)
-    rows, features = pts_ref.shape
-    vectors = vec_ref.shape[1]
+    features, rows = pts_ref.shape
+    vectors = vec_ref.shape[0]
+    side = square_side(nrow)
+    high_row, low_row = row // side, row % side
     stacks = packing(rows)
     high = rows // stacks
     per_tile = max(1, LANES // features)
 
     def row_at(j):
-        return lax.rem(row + j, nrow)
+        return lax.rem(high_row + j // side, nrow // side) * side + lax.rem(low_row + j % side, side)
+
+    straight = [j for j in range(1, nrow) if j // side == 0 or j % side == 0]
+    oblique = [j for j in range(1, nrow) if j // side and j % side]
 
     def col_at(k):
         return lax.rem(z + k, nz) * 2 + core
@@ -78,29 +99,51 @@
         )
 
     def arrived(gather, r, c):
-        buf, recv, along, spread, pair = gather
+        buf, recv, along, spread, pair, onward, routed = gather
         block(buf, r, c, pair.at[0, 0], recv, row, sibling).wait_recv()
 
     def hand_over(gather, j, k):
-        buf, recv, along, spread, pair = gather
+        buf, recv, along, spread, pair, onward, routed = gather
         block(buf, row_at(j), col_at(k), pair.at[j, k], recv, row, sibling).start()
 
     def send_plane(gather, k):
-        buf, recv, along, spread, pair = gather
-        for j in range(1, nrow):
-            block(buf, row, col_at(k), spread.at[k, j - 1], recv, row_at(j), col).start()
+        buf, recv, along, spread, pair, onward, routed = gather
+        for j in straight + (oblique if routed else []):
+            block(buf, row, col_at(k), spread.at[k, j], recv, row_at(j), col).start()
         hand_over(gather, 0, k)
 
+    def relays(gather, j, k):
+        buf, recv, along, spread, pair, onward, routed = gather
+        copies = []
+        if routed:
+            targets = []
+        elif j // side == 0 and k % 2 == 0:
+            targets = [d * side for d in range(1, nrow // side)]
+        elif j % side == 0 and k % 2 == 1:
+            targets = range(1, side)
+        else:
+            targets = []
+        return [
+            block(buf, row_at(j), col_at(k), onward.at[j, k, i], recv, row_at(t), col)
+            for i, t in enumerate(targets)
+        ]
+
+    def relay(gather, k):
+        for j in straight:
+            arrived(gather, row_at(j), col_at(k))
+            for copy in relays(gather, j, k):
+                copy.start()
+            hand_over(gather, j, k)
+
     def send_own(gather):
-        buf, recv, along, spread, pair = gather
+        buf, recv, along, spread, pair, onward, routed = gather
         for k in range(1, nz):
             block(buf, row, col, along.at[k - 1], recv, row, col_at(k)).start()
         send_plane(gather, 0)
 
-    def pass_on(gather):
-        for k in range(1, nz):
-            arrived(gather, row, col_at(k))
-            send_plane(gather, k)
+    def pass_on(gather, k):
+        arrived(gather, row, col_at(k))
+        send_plane(gather, k)
 
     def hand_over_row(gather, j):
         for k in range(nz):
@@ -112,18 +155,20 @@
             arrived(gather, row_at(j), lax.rem(z + k, nz) * 2 + (1 - core))
 
     def drain(gather):
-        buf, recv, along, spread, pair = gather
+        buf, recv, along, spread, pair, onward, routed = gather
         for k in range(1, nz):
             block(buf, row, col, along.at[k - 1], recv, row, col_at(k)).wait_send()
         for k in range(nz):
-            for j in range(1, nrow):
-                block(buf, row, col_at(k), spread.at[k, j - 1], recv, row_at(j), col).wait_send()
+            for j in straight + (oblique if routed else []):
+                block(buf, row, col_at(k), spread.at[k, j], recv, row_at(j), col).wait_send()
+                for copy in relays(gather, j, k):
+                    copy.wait_send()
             for j in range(nrow):
                 block(buf, row_at(j), col_at(k), pair.at[j, k], recv, row, sibling).wait_send()
 
-    points = (gp,) + tuple(sems_p)
-    start = (gv,) + tuple(sems_v)
-    middle = (gs,) + tuple(sems_s)
+    points = (gp,) + tuple(sems_p) + (False,)
+    start = (gv,) + tuple(sems_v) + (False,)
+    middle = (gs,) + tuple(sems_s) + (True,)
 
     barrier = pltpu.get_barrier_semaphore()
     for j in range(1, nrow):
@@ -132,9 +177,9 @@
         pl.semaphore_signal(barrier, inc=1, device_id=(row, lax.rem(col + k, ncol)), device_id_type=MESH)
 
     own = pl.ds(pl.multiple_of(col * high, high), high)
-    x = pts_ref[...]
+    x = upright(pts_ref[...])
     gp[row, own, :] = side_by_side(x, stacks)
-    gv[row, own, :] = side_by_side(vec_ref[...], stacks)
+    gv[row, own, :] = side_by_side(upright(vec_ref[...]), stacks)
     pl.semaphore_wait(barrier, nrow + ncol - 2)
 
     send_own(points)
@@ -170,37 +215,42 @@
             power = (cross * (-2.0 * rate) + there[8 * part : 8 * part + 1]) + here
             aff[r, s] = jnp.exp2(power).astype(jnp.bfloat16)
 
-    pass_on(points)
-    pass_on(start)
+    for k in range(1, nz):
+        pass_on(points, k)
+        pass_on(start, k)
+        relay(points, k - 1)
+    relay(points, nz - 1)
     sibling_row(points, 0)
     weights(row)
-
-    def next_row(j, carry):
-        hand_over_row(points, j)
+    for k in range(nz):
+        relay(start, k)
+    for j in straight:
         sibling_row(points, j)
         weights(row_at(j))
-        return carry
-
-    lax.fori_loop(1, nrow, next_row, 0)
+        if j == straight[0]:
+            for o in oblique:
+                hand_over_row(points, o)
+    for j in oblique:
+        sibling_row(points, j)
+        weights(row_at(j))
 
     span = gv.shape[2]
     ones = jnp.ones((ncol * high, LANES), jnp.bfloat16)
     acc[...] = jnp.zeros_like(acc)
 
-    def first_row(j, carry):
+    def first_row(j):
         sibling_row(start, j)
         r = row_at(j)
         panel = jnp.concatenate([gv[r], ones], axis=1)
         for s in range(stacks):
             acc[s] += jnp.dot(aff[r, s], panel, preferred_element_type=jnp.float32)
-        return carry
-
-    def hand_over_start(j, carry):
+
+    for j in [0] + straight:
+        first_row(j)
+    for j in oblique:
         hand_over_row(start, j)
-        return carry
-
-    lax.fori_loop(1, nrow, hand_over_start, 0)
-    lax.fori_loop(0, nrow, first_row, 0)
+    for j in oblique:
+        first_row(j)
 
     product = sum(acc[s][:, s * vectors : (s + 1) * vectors] for s in range(stacks))
     degree = sum(acc[s][:, span : span + vectors] for s in range(stacks))
@@ -244,38 +294,42 @@
         for j in range(1, nrow):
             gram_copy(gram_row, step, row, j - 1, row_at(j), col, 1).wait_send()
 
-    gram_send(0, scaled)
-    pass_on(middle)
-    gram_across(0)
-    first = inverse_factor(gram_whole(0))
-
-    def hand_over_middle(j, carry):
-        hand_over_row(middle, j)
-        return carry
-
-    def second_row(j, carry):
+    for k in range(1, nz):
+        pass_on(middle, k)
+        relay(middle, k - 1)
+    relay(middle, nz - 1)
+    mixed = jnp.zeros((span, span), jnp.float32)
+    acc[...] = jnp.zeros_like(acc)
+
+    def second_row(j):
         sibling_row(middle, j)
         r = row_at(j)
         for s in range(stacks):
             acc[s, :, :span] += jnp.dot(aff[r, s], gs[r], preferred_element_type=jnp.float32)
-        return carry
-
-    acc[...] = jnp.zeros_like(acc)
-    lax.fori_loop(1, nrow, hand_over_middle, 0)
-    lax.fori_loop(0, nrow, second_row, 0)
+        return mixed + jnp.dot(upright(gs[r]), gs[r], preferred_element_type=jnp.float32)
+
+    for j in [0] + straight:
+        mixed = second_row(j)
+    for j in oblique:
+        hand_over_row(middle, j)
+    for j in oblique:
+        mixed = second_row(j)
+    gram = sum(
+        mixed[s * vectors : (s + 1) * vectors, s * vectors : (s + 1) * vectors] for s in range(stacks)
+    )
+    first = inverse_factor(gram * (1.0 / total))
     product = sum(acc[s][:, s * vectors : (s + 1) * vectors] for s in range(stacks))
     scaled = lax.dot_general(
         product / degree, first, contract, precision=HIGHEST, preferred_element_type=jnp.float32
     )
-    gram_send(1, scaled)
+    gram_send(0, scaled)
     drain(points)
     drain(start)
     drain(middle)
+    gram_across(0)
+    second = inverse_factor(gram_whole(0))
+    out_ref[...] = lax.dot_general(second, scaled, contract, precision=HIGHEST, preferred_element_type=jnp.float32)
     gram_drain(0)
-    gram_across(1)
-    second = inverse_factor(gram_whole(1))
-    out_ref[...] = lax.dot_general(scaled, second, contract, precision=HIGHEST, preferred_element_type=jnp.float32)
-    gram_drain(1)
 
 
 def solution(mesh):
@@ -289,11 +343,11 @@
         high = rows // stacks
         wide, span = width(stacks, features), width(stacks, vectors)
         dma = pltpu.SemaphoreType.DMA
-        gather = [dma((nrow, ncol)), dma((nz,)), dma((nz, nrow)), dma((nrow, nz))]
+        gather = [dma((nrow, ncol)), dma((nz,)), dma((nz, nrow)), dma((nrow, nz)), dma((nrow, nz, square_side(nrow)))]
         tall = vectors * vectors // LANES
         return pl.pallas_call(
             functools.partial(kernel, nrow, ncol, rows * nrow * ncol),
-            out_shape=jax.ShapeDtypeStruct((rows, vectors), jnp.float32),
+            out_shape=jax.ShapeDtypeStruct((vectors, rows), jnp.float32),
             in_specs=[pl.BlockSpec(memory_space=pltpu.VMEM)] * 2,
             out_specs=pl.BlockSpec(memory_space=pltpu.VMEM),
             scratch_shapes=[
@@ -302,15 +356,15 @@
                 pltpu.VMEM((nrow, ncol * high, span), jnp.bfloat16),
                 pltpu.VMEM((nrow, stacks, rows, ncol * high), jnp.bfloat16),
                 pltpu.VMEM((stacks, rows, span + LANES), jnp.float32),
-                pltpu.VMEM((2, ncol, tall, LANES), jnp.float32),
-                pltpu.VMEM((2, nrow, tall, LANES), jnp.float32),
+                pltpu.VMEM((1, ncol, tall, LANES), jnp.float32),
+                pltpu.VMEM((1, nrow, tall, LANES), jnp.float32),
                 gather, gather, gather,
-                [dma((2, ncol)), dma((2, ncol)), dma((2, nrow)), dma((2, nrow))],
+                [dma((1, ncol)), dma((1, ncol)), dma((1, nrow)), dma((1, nrow))],
             ],
             compiler_params=pltpu.CompilerParams(
                 collective_id=0, has_side_effects=True, vmem_limit_bytes=56 * 1024 * 1024
             ),
-        )(points, start_vectors)
+        )(points.T, start_vectors.T).T
 
     return jax.shard_map(
         step,

time: 60.5 us -> 55.2 us (0.912)
  Pallas kernels: 56.3 us -> 53.6 us
  local copies, waits for them, and re-layouts: 3.92 us -> 1.42 us
    pallas_call x1, Pallas kernels: 56.3 us -> 53.6 us  [step(): pl.pallas_call(functools.partial(kernel, nrow, ncol, rows * nrow * ncol),...]
    pallas_call x1 -> x0, local copies, waits for them, and re-layouts: 1.64 us -> none  [step(): pl.pallas_call(functools.partial(kernel, nrow, ncol, rows * nrow * ncol),...]
    unnamed x4 -> x1, local copies, waits for them, and re-layouts: 2.28 us -> 1.42 us
where the time goes in v2:
time: 55.2 us; the launch traced here: 55 us
  Pallas kernels  53.6 us (97%)
  local copies, waits for them, and re-layouts  1.42 us (3%)
    pallas_call x1, Pallas kernels, step(): pl.pallas_call(functools.partial(kernel, nrow, ncol, rows * nrow * ncol),...  53.6 us
    unnamed x1, local copies, waits for them, and re-layouts  1.42 us

profile of v2, /device:TPU:0, one launch (start us, length us, event | category | flops | bytes accessed | tf_op | source)
XLA Modules:
  0.0 55.0 jit_solution(15666225939621838784)
XLA Ops:
  0.0 53.6 %shard_map.28 = f32[32,320]{1,0:T(8,128)} custom-call(bf16[64,320]{1,0:T(8,128)(2,1)} %bitcast.4, bf16[32,320]{1,0:T(8,128)(2,1)} %bitcast.5), custom_call_target="tpu_custom_call" | custom-call | tf_op jit(solution)/shard_map/pallas_call | solution.py:348
  53.6 1.4 %copy.4 = f32[320,32]{0,1:T(8,128)} copy(f32[320,32]{0,1:T(8,128)} %bitcast.3) | data formatting | bytes 81920

commit v3 on v2

--- a/solution.py
+++ b/solution.py
@@ -245,10 +245,10 @@
         for s in range(stacks):
             acc[s] += jnp.dot(aff[r, s], panel, preferred_element_type=jnp.float32)
 
+    for j in oblique:
+        hand_over_row(start, j)
     for j in [0] + straight:
         first_row(j)
-    for j in oblique:
-        hand_over_row(start, j)
     for j in oblique:
         first_row(j)
 
@@ -308,10 +308,10 @@
             acc[s, :, :span] += jnp.dot(aff[r, s], gs[r], preferred_element_type=jnp.float32)
         return mixed + jnp.dot(upright(gs[r]), gs[r], preferred_element_type=jnp.float32)
 
+    for j in oblique:
+        hand_over_row(middle, j)
     for j in [0] + straight:
         mixed = second_row(j)
-    for j in oblique:
-        hand_over_row(middle, j)
     for j in oblique:
         mixed = second_row(j)
     gram = sum(

time: 55.2 us -> 53.8 us (0.975)
  Pallas kernels: 53.6 us -> 52.1 us
    pallas_call x1, Pallas kernels: 53.6 us -> 52.1 us  [step(): pl.pallas_call(functools.partial(kernel, nrow, ncol, rows * nrow * ncol),...]
where the time goes in v3:
time: 53.8 us; the launch traced here: 53.6 us
  Pallas kernels  52.1 us (97%)
  local copies, waits for them, and re-layouts  1.42 us (3%)
    pallas_call x1, Pallas kernels, step(): pl.pallas_call(functools.partial(kernel, nrow, ncol, rows * nrow * ncol),...  52.1 us
    unnamed x1, local copies, waits for them, and re-layouts  1.42 us

profile of v3, /device:TPU:0, one launch (start us, length us, event | category | flops | bytes accessed | tf_op | source)
XLA Modules:
  0.0 53.6 jit_solution(10052674913847566159)
XLA Ops:
  0.0 52.1 %shard_map.28 = f32[32,320]{1,0:T(8,128)} custom-call(bf16[64,320]{1,0:T(8,128)(2,1)} %bitcast.4, bf16[32,320]{1,0:T(8,128)(2,1)} %bitcast.5), custom_call_target="tpu_custom_call" | custom-call | tf_op jit(solution)/shard_map/pallas_call | solution.py:348
  52.1 1.4 %copy.4 = f32[320,32]{0,1:T(8,128)} copy(f32[320,32]{0,1:T(8,128)} %bitcast.3) | data formatting | bytes 81920
